TPU v7x, 32 devices: a whole 2x2x4 slice. The times are simulated.
32 devices in a mesh: depth: 8 (over z, x), tile: 4 (over y, core).
Axes of the slice: x: 2, y: 2, z: 4, core: 2. Of those that a mesh axis runs over, the one named last changes fastest.
Arguments:
- volume: bfloat16 [64, 256, 4096], P('depth', 'tile'), may hold values from -6 to 6
- shear: int32 [64], replicated, may hold values from -64 to 64, as said below
- footprint: int32 [8, 2], P('depth'), may hold values from 0 to 4096, as said below
Outputs:
- frame: float32 [4, 256, 4096], P(None, 'tile', 'depth')
Inputs may be any that keep to these rules, and one draw needn't show every extreme that they name: Offsets follow a linear tilt over the slices with small jitter; shear[0] and shear[63] are the two ends of the range, in either order. footprint[b, 0] < 1024 and footprint[b, 1] > 3072 for every brick.
All inputs are finite; a program needn't handle non-finite values.
Results may differ from a plain program's by a relative error of at most 0.00085.
Values may be sent and summed in bfloat16 or wider, within the bound.
No kernel may reach another device: no remote copies, remote signals or barrier semaphores. Data moves between devices by JAX's collectives and lax.ppermute only.
A program may use at most 64 MiB of HBM per device.

v0:
```python
import jax
import jax.numpy as jnp
from jax import lax
from jax.sharding import PartitionSpec as P

NY = 4096
SMAX = 64


def extended_2(x, sides, width):
    for axis, dim in sides:
        count, length = (lax.axis_size(axis), x.shape[dim])
        up = [(i, (i + 1) % count) for i in range(count - 1)]
        down = [(j, i) for i, j in up]
        last = lax.slice_in_dim(x, length - width, length, axis=dim)
        leading = lax.slice_in_dim(x, 0, width, axis=dim)
        before = lax.ppermute(last, axis, up)
        after = lax.ppermute(leading, axis, down)
        x = jnp.concatenate([before, x, after], axis=dim)
    return x


def colour(cur, gx, gy, gz, offset, low, high, absorb):
    norm = jnp.sqrt(gx * gx + gy * gy + gz * gz + 1.0)
    shade = 0.3 + 0.7 * jnp.abs(0.48 * gx + 0.6 * gy + 0.64 * gz) / norm
    alpha = 1.0 - jnp.exp(-absorb * cur * cur)
    rgba = jnp.stack(
        [
            shade * jax.nn.sigmoid(1.2 * cur + 0.2) * alpha,
            shade * jax.nn.sigmoid(-0.8 * cur) * alpha,
            shade * jax.nn.sigmoid(0.5 * cur - 0.3) * alpha,
            alpha,
        ]
    )
    padded = jnp.pad(rgba, ((0, 0), (0, 0), (SMAX, SMAX)))
    moved = lax.dynamic_slice_in_dim(padded, SMAX - offset, NY, 2)
    column = jnp.arange(NY, dtype=jnp.int32)
    inside = ((column >= low) & (column < high)).astype(jnp.float32)
    return moved * inside


def shards(volume, shear, footprint):
    slices = volume.shape[0]
    rows = volume.shape[1]
    bricks = lax.axis_size("depth")
    total = slices * bricks
    absorb = 2.0 / total
    flip = shear[0] > shear[total - 1]
    me = lax.axis_index("depth")
    local_shear = lax.dynamic_slice_in_dim(shear, me * slices, slices, 0)
    extended = extended_2(volume, (("depth", 0), ("tile", 1)), 1)

    def slice_step(step, acc):
        local = jnp.where(flip, slices - 1 - step, step).astype(jnp.int32)
        block = lax.dynamic_slice_in_dim(extended, local, 3, 0).astype(jnp.float32)
        cur = block[1, 1:-1]
        gz = 0.5 * (block[2, 1:-1] - block[0, 1:-1])
        gx = 0.5 * (block[1, 2:] - block[1, :-2])
        cols = jnp.pad(cur, ((0, 0), (1, 1)))
        gy = 0.5 * (cols[:, 2:] - cols[:, :-2])
        placed = colour(
            cur, gx, gy, gz, local_shear[local], footprint[0, 0], footprint[0, 1], absorb
        )
        return acc + (1.0 - acc[3:4]) * placed

    acc = lax.fori_loop(0, slices, slice_step, jnp.zeros((4, rows, NY), jnp.float32))
    partial_value = acc.astype(jnp.bfloat16)
    pieces = lax.all_to_all(partial_value[None], "depth", split_axis=3, concat_axis=0, tiled=True)

    def brick_step(position, image):
        source = jnp.where(flip, bricks - 1 - position, position).astype(jnp.int32)
        piece = lax.dynamic_index_in_dim(pieces, source, 0, keepdims=False).astype(jnp.float32)
        return image + (1.0 - image[3:4]) * piece

    start = jnp.zeros(pieces.shape[1:], jnp.float32)
    return lax.fori_loop(0, bricks, brick_step, start)


def solution(mesh):
    placed = (P("depth", "tile", None), P(), P("depth", None))
    return jax.shard_map(
        shards, mesh=mesh, in_specs=placed, out_specs=P(None, "tile", "depth"), check_vma=False
    )
```

profile of v0, /device:TPU:1, one launch (start us, length us, event | category | flops | bytes accessed | tf_op | source)
XLA Modules:
  0.0 268.8 jit_solution(5925467425739162417)
XLA Ops:
  1.3 4.0 %collective-permute-start = (bf16[1,64,4096]{2,1,0:T(8,128)(2,1)S(1)}, bf16[1,64,4096]{2,1,0:T(8,128)(2,1)S(1)}, u32[]{:S(2)}, u32[]{:S(2)}) collective-permute-start(bf16[1,64,4096]{2,1,0:T(8,128)(2,1)S(1)} %get-tuple-element.320), channel_id=1, source_target_pairs={{0,4},{4,8},{8,12},{12,16},{16,20},{20,24},{24,28},{1,5},{5,9},{9,... | collective-permute-start | bytes 1572872 | tf_op jit(solution)/shard_map/ppermute | solution.py:17
  7.3 19.7 %collective-permute-done = bf16[1,64,4096]{2,1,0:T(8,128)(2,1)S(1)} collective-permute-done((bf16[1,64,4096]{2,1,0:T(8,128)(2,1)S(1)}, bf16[1,64,4096]{2,1,0:T(8,128)(2,1)S(1)}, u32[]{:S(2)}, u32[]{:S(2)}) %collective-permute-start) | collective-permute-done | bytes 524320 | tf_op jit(solution)/shard_map/ppermute | solution.py:17
  30.0 4.6 %collective-permute-start.2 = (bf16[10,1,4096]{2,1,0:T(2,128)(2,1)S(1)}, bf16[10,1,4096]{2,1,0:T(2,128)(2,1)S(1)}, u32[]{:S(2)}, u32[]{:S(2)}) collective-permute-start(bf16[10,1,4096]{2,1,0:T(2,128)(2,1)S(1)} %get-tuple-element.317), channel_id=1, source_target_pairs={{0,1},{1,2},{2,3},{4,5},{5,6},{6,7},{8,9},{9,10},{10,11},{12,13},{... | collective-permute-start | bytes 245768 | tf_op jit(solution)/shard_map/ppermute | solution.py:17
  38.3 2.9 %collective-permute-done.3 = bf16[10,1,4096]{2,1,0:T(2,128)(2,1)S(1)} collective-permute-done((bf16[10,1,4096]{2,1,0:T(2,128)(2,1)S(1)}, bf16[10,1,4096]{2,1,0:T(2,128)(2,1)S(1)}, u32[]{:S(2)}, u32[]{:S(2)}) %collective-permute-start.3) | collective-permute-done | bytes 81952 | tf_op jit(solution)/shard_map/ppermute | solution.py:18
  41.2 6.1 %pad_maximum_fusion = bf16[10,66,4096]{2,1,0:T(8,128)(2,1)} fusion(bf16[10,1,4096]{2,1,0:T(2,128)(2,1)S(1)} %collective-permute-done.3, bf16[10,64,4096]{2,1,0:T(8,128)(2,1)S(1)} %constant_dynamic-update-slice_fusion, bf16[10,1,4096]{2,1,0:T(2,128)(2,1)S(1)} %collective-permute-done.2), kind=kLoop, calls=%fused_computation.53 | loop fusion | flops 16220160 | bytes 10813440 | tf_op jit(solution)/shard_map/concatenate | solution.py:19
  47.3 135.7 %while.30 = (s32[]{:T(128)}, f32[4,64,4096]{2,1,0:T(8,128)}, pred[]{:T(512)}, bf16[10,66,4096]{2,1,0:T(8,128)(2,1)}, s32[8]{0:T(128)S(1)}, /*index=5*/s32[1,2]{1...) while((s32[]{:T(128)}, f32[4,64,4096]{2,1,0:T(8,128)}, ...), condition=%wide.region_1.2_spmd.clone, body=%wide.region_0.1_spmd.clone.sunk | while | flops 30973964 | bytes 48940876 | solution.py:66
  49.4 2.5 multiply_bitcast_fusion.5
  57.0 3.9 %fusion.44 = f32[4,64,4096]{2,1,0:T(8,128)} fusion(s32[]{:T(128)S(6)} %select_n.74, f32[1,64,4096]{2,1,0:T(8,128)S(1)} %get-tuple-element.391, f32[1,64,4096]{2,1,0:T(8,128)S(1)} %get-tuple-element.392, f32[1,64,4096]{2,1,0:T(8,128)S(1)} %copy-done, f32[1,64,4096]{2,1,0:T(8,128)S(1)} %get-tuple-element.394, f32[4096]{0:T(1024)S(1)} %fusion.42, ...), kind=kLoop, calls=%fused_computation.10.clone.1 | loop fusion | flops 15728640 | bytes 13649408 | tf_op jit(solution)/shard_map/while/body/eval_jaxpr/add | solution.py:64
  63.1 2.5 multiply_bitcast_fusion.5
  68.2 2.6 broadcast_select_fusion.4
  72.9 5.4 %fusion.44 = f32[4,64,4096]{2,1,0:T(8,128)} fusion(s32[]{:T(128)S(6)} %select_n.74, f32[1,64,4096]{2,1,0:T(8,128)S(1)} %get-tuple-element.391, f32[1,64,4096]{2,1,0:T(8,128)S(1)} %get-tuple-element.392, f32[1,64,4096]{2,1,0:T(8,128)S(1)} %copy-done, f32[1,64,4096]{2,1,0:T(8,128)S(1)} %get-tuple-element.394, f32[4096]{0:T(1024)S(1)} %fusion.42, ...), kind=kLoop, calls=%fused_computation.10.clone.1 | loop fusion | flops 15728640 | bytes 13649408 | tf_op jit(solution)/shard_map/while/body/eval_jaxpr/add | solution.py:64
  80.5 2.5 multiply_bitcast_fusion.5
  85.7 2.6 broadcast_select_fusion.4
  90.3 5.4 %fusion.44 = f32[4,64,4096]{2,1,0:T(8,128)} fusion(s32[]{:T(128)S(6)} %select_n.74, f32[1,64,4096]{2,1,0:T(8,128)S(1)} %get-tuple-element.391, f32[1,64,4096]{2,1,0:T(8,128)S(1)} %get-tuple-element.392, f32[1,64,4096]{2,1,0:T(8,128)S(1)} %copy-done, f32[1,64,4096]{2,1,0:T(8,128)S(1)} %get-tuple-element.394, f32[4096]{0:T(1024)S(1)} %fusion.42, ...), kind=kLoop, calls=%fused_computation.10.clone.1 | loop fusion | flops 15728640 | bytes 13649408 | tf_op jit(solution)/shard_map/while/body/eval_jaxpr/add | solution.py:64
  103.1 2.6 broadcast_select_fusion.4
  107.8 5.4 %fusion.44 = f32[4,64,4096]{2,1,0:T(8,128)} fusion(s32[]{:T(128)S(6)} %select_n.74, f32[1,64,4096]{2,1,0:T(8,128)S(1)} %get-tuple-element.391, f32[1,64,4096]{2,1,0:T(8,128)S(1)} %get-tuple-element.392, f32[1,64,4096]{2,1,0:T(8,128)S(1)} %copy-done, f32[1,64,4096]{2,1,0:T(8,128)S(1)} %get-tuple-element.394, f32[4096]{0:T(1024)S(1)} %fusion.42, ...), kind=kLoop, calls=%fused_computation.10.clone.1 | loop fusion | flops 15728640 | bytes 13649408 | tf_op jit(solution)/shard_map/while/body/eval_jaxpr/add | solution.py:64
  120.6 2.6 broadcast_select_fusion.4
  125.2 5.4 %fusion.44 = f32[4,64,4096]{2,1,0:T(8,128)} fusion(s32[]{:T(128)S(6)} %select_n.74, f32[1,64,4096]{2,1,0:T(8,128)S(1)} %get-tuple-element.391, f32[1,64,4096]{2,1,0:T(8,128)S(1)} %get-tuple-element.392, f32[1,64,4096]{2,1,0:T(8,128)S(1)} %copy-done, f32[1,64,4096]{2,1,0:T(8,128)S(1)} %get-tuple-element.394, f32[4096]{0:T(1024)S(1)} %fusion.42, ...), kind=kLoop, calls=%fused_computation.10.clone.1 | loop fusion | flops 15728640 | bytes 13649408 | tf_op jit(solution)/shard_map/while/body/eval_jaxpr/add | solution.py:64
  138.0 2.6 broadcast_select_fusion.4
  142.7 5.4 %fusion.44 = f32[4,64,4096]{2,1,0:T(8,128)} fusion(s32[]{:T(128)S(6)} %select_n.74, f32[1,64,4096]{2,1,0:T(8,128)S(1)} %get-tuple-element.391, f32[1,64,4096]{2,1,0:T(8,128)S(1)} %get-tuple-element.392, f32[1,64,4096]{2,1,0:T(8,128)S(1)} %copy-done, f32[1,64,4096]{2,1,0:T(8,128)S(1)} %get-tuple-element.394, f32[4096]{0:T(1024)S(1)} %fusion.42, ...), kind=kLoop, calls=%fused_computation.10.clone.1 | loop fusion | flops 15728640 | bytes 13649408 | tf_op jit(solution)/shard_map/while/body/eval_jaxpr/add | solution.py:64
  155.5 2.6 broadcast_select_fusion.4
  160.1 5.4 %fusion.44 = f32[4,64,4096]{2,1,0:T(8,128)} fusion(s32[]{:T(128)S(6)} %select_n.74, f32[1,64,4096]{2,1,0:T(8,128)S(1)} %get-tuple-element.391, f32[1,64,4096]{2,1,0:T(8,128)S(1)} %get-tuple-element.392, f32[1,64,4096]{2,1,0:T(8,128)S(1)} %copy-done, f32[1,64,4096]{2,1,0:T(8,128)S(1)} %get-tuple-element.394, f32[4096]{0:T(1024)S(1)} %fusion.42, ...), kind=kLoop, calls=%fused_computation.10.clone.1 | loop fusion | flops 15728640 | bytes 13649408 | tf_op jit(solution)/shard_map/while/body/eval_jaxpr/add | solution.py:64
  172.9 2.6 broadcast_select_fusion.4
  177.6 5.4 %fusion.44 = f32[4,64,4096]{2,1,0:T(8,128)} fusion(s32[]{:T(128)S(6)} %select_n.74, f32[1,64,4096]{2,1,0:T(8,128)S(1)} %get-tuple-element.391, f32[1,64,4096]{2,1,0:T(8,128)S(1)} %get-tuple-element.392, f32[1,64,4096]{2,1,0:T(8,128)S(1)} %copy-done, f32[1,64,4096]{2,1,0:T(8,128)S(1)} %get-tuple-element.394, f32[4096]{0:T(1024)S(1)} %fusion.42, ...), kind=kLoop, calls=%fused_computation.10.clone.1 | loop fusion | flops 15728640 | bytes 13649408 | tf_op jit(solution)/shard_map/while/body/eval_jaxpr/add | solution.py:64
  185.5 4.7 %copy.10 = bf16[4,64,4096]{1,0,2:T(4,128)(2,1)} copy(bf16[4,64,4096]{2,1,0:T(8,128)(2,1)S(1)} %convert_element_type.52) | data formatting | bytes 4194304
  190.2 5.3 %bitcast_bitcast_fusion = bf16[4096,1,4,64]{3,2,1,0:T(4,128)(2,1)} fusion(bf16[4,64,4096]{1,0,2:T(4,128)(2,1)} %copy.10), kind=kLoop, calls=%fused_computation.61 | loop fusion | bytes 4194304
  195.5 7.6 %reshape.29 = bf16[8,2,65536]{2,1,0:T(2,128)(2,1)} reshape(bf16[4096,1,4,64]{3,2,1,0:T(4,128)(2,1)} %bitcast_bitcast_fusion) | data formatting | bytes 4194304
  203.1 5.5 %all-to-all-start = ((bf16[8,2,65536]{2,1,0:T(2,128)(2,1)}), bf16[8,2,65536]{2,1,0:T(2,128)(2,1)S(1)}, u32[]{:S(2)}, u32[]{:S(2)}) async-start(bf16[8,2,65536]{2,1,0:T(2,128)(2,1)} %reshape.29), calls=%async_computation | async-start | bytes 4194304 | tf_op jit(solution)/shard_map/all_to_all | solution.py:68
  208.6 46.3 %all-to-all-done = bf16[8,2,65536]{2,1,0:T(2,128)(2,1)S(1)} async-done(((bf16[8,2,65536]{2,1,0:T(2,128)(2,1)}), bf16[8,2,65536]{2,1,0:T(2,128)(2,1)S(1)}, u32[]{:S(2)}, u32[]{:S(2)}) %all-to-all-start) | async-done | bytes 2097184 | tf_op jit(solution)/shard_map/all_to_all | solution.py:68
  254.9 5.0 %reshape.30 = bf16[4096,1,4,64]{3,2,1,0:T(4,128)(2,1)} reshape(bf16[8,2,65536]{2,1,0:T(2,128)(2,1)S(1)} %all-to-all-done) | data formatting | bytes 4194304
  259.9 5.6 %copy.9 = bf16[1,4,64,8,512]{4,2,1,3,0:T(8,128)(2,1)S(1)} copy(bf16[1,4,64,8,512]{2,1,4,3,0:T(4,128)(2,1)} %bitcast.87) | data formatting | bytes 4194304 | tf_op jit(solution)/shard_map/all_to_all | solution.py:68
  265.5 2.5 while.31
  (122 shorter events, 71.5 us)
Async XLA Ops:
  1.3 25.8 %collective-permute-start = (bf16[1,64,4096]{2,1,0:T(8,128)(2,1)S(1)}, bf16[1,64,4096]{2,1,0:T(8,128)(2,1)S(1)}, u32[]{:S(2)}, u32[]{:S(2)}) collective-permute-start(bf16[1,64,4096]{2,1,0:T(8,128)(2,1)S(1)} %get-tuple-element.320), channel_id=1, source_target_pairs={{0,4},{4,8},{8,12},{12,16},{16,20},{20,24},{24,28},{1,5},{5,9},{9,... | collective-permute-start | bytes 1572872 | tf_op jit(solution)/shard_map/ppermute | solution.py:17
  5.2 24.3 %collective-permute-start.1 = (bf16[1,64,4096]{2,1,0:T(8,128)(2,1)S(1)}, bf16[1,64,4096]{2,1,0:T(8,128)(2,1)S(1)}, u32[]{:S(2)}, u32[]{:S(2)}) collective-permute-start(bf16[1,64,4096]{2,1,0:T(8,128)(2,1)S(1)} %get-tuple-element.319), channel_id=1, source_target_pairs={{4,0},{8,4},{12,8},{16,12},{20,16},{24,20},{28,24},{5,1},{9,5},{13... | collective-permute-start | bytes 1572872 | tf_op jit(solution)/shard_map/ppermute | solution.py:18
  27.1 9.4 %copy-start.3 = (s32[64]{0:T(128)S(1)}, s32[64]{0:T(128)}, u32[]{:S(2)}) copy-start(s32[64]{0:T(128)} %param.8) | copy-start | bytes 772
  30.0 8.3 %collective-permute-start.2 = (bf16[10,1,4096]{2,1,0:T(2,128)(2,1)S(1)}, bf16[10,1,4096]{2,1,0:T(2,128)(2,1)S(1)}, u32[]{:S(2)}, u32[]{:S(2)}) collective-permute-start(bf16[10,1,4096]{2,1,0:T(2,128)(2,1)S(1)} %get-tuple-element.317), channel_id=1, source_target_pairs={{0,1},{1,2},{2,3},{4,5},{5,6},{6,7},{8,9},{9,10},{10,11},{12,13},{... | collective-permute-start | bytes 245768 | tf_op jit(solution)/shard_map/ppermute | solution.py:17
  34.5 6.6 %collective-permute-start.3 = (bf16[10,1,4096]{2,1,0:T(2,128)(2,1)S(1)}, bf16[10,1,4096]{2,1,0:T(2,128)(2,1)S(1)}, u32[]{:S(2)}, u32[]{:S(2)}) collective-permute-start(bf16[10,1,4096]{2,1,0:T(2,128)(2,1)S(1)} %get-tuple-element.318), channel_id=1, source_target_pairs={{1,0},{2,1},{3,2},{5,4},{6,5},{7,6},{9,8},{10,9},{11,10},{13,12},{... | collective-permute-start | bytes 245768 | tf_op jit(solution)/shard_map/ppermute | solution.py:18
  38.3 9.0 %copy-start.2 = (s32[1,2]{1,0:T(1,128)S(1)}, s32[1,2]{1,0:T(1,128)}, u32[]{:S(2)}) copy-start(s32[1,2]{1,0:T(1,128)} %param.9) | copy-start | bytes 28
  54.6 2.4 copy-start
  68.2 4.7 %copy-start = (f32[1,64,4096]{2,1,0:T(8,128)S(1)}, f32[1,64,4096]{2,1,0:T(8,128)}, u32[]{:S(2)}) copy-start(f32[1,64,4096]{2,1,0:T(8,128)} %get-tuple-element.393) | copy-start | bytes 3145732 | tf_op jit(solution)/shard_map/while
  85.7 4.7 %copy-start = (f32[1,64,4096]{2,1,0:T(8,128)S(1)}, f32[1,64,4096]{2,1,0:T(8,128)}, u32[]{:S(2)}) copy-start(f32[1,64,4096]{2,1,0:T(8,128)} %get-tuple-element.393) | copy-start | bytes 3145732 | tf_op jit(solution)/shard_map/while
  103.1 4.7 %copy-start = (f32[1,64,4096]{2,1,0:T(8,128)S(1)}, f32[1,64,4096]{2,1,0:T(8,128)}, u32[]{:S(2)}) copy-start(f32[1,64,4096]{2,1,0:T(8,128)} %get-tuple-element.393) | copy-start | bytes 3145732 | tf_op jit(solution)/shard_map/while
  120.6 4.7 %copy-start = (f32[1,64,4096]{2,1,0:T(8,128)S(1)}, f32[1,64,4096]{2,1,0:T(8,128)}, u32[]{:S(2)}) copy-start(f32[1,64,4096]{2,1,0:T(8,128)} %get-tuple-element.393) | copy-start | bytes 3145732 | tf_op jit(solution)/shard_map/while
  138.0 4.7 %copy-start = (f32[1,64,4096]{2,1,0:T(8,128)S(1)}, f32[1,64,4096]{2,1,0:T(8,128)}, u32[]{:S(2)}) copy-start(f32[1,64,4096]{2,1,0:T(8,128)} %get-tuple-element.393) | copy-start | bytes 3145732 | tf_op jit(solution)/shard_map/while
  155.4 4.7 %copy-start = (f32[1,64,4096]{2,1,0:T(8,128)S(1)}, f32[1,64,4096]{2,1,0:T(8,128)}, u32[]{:S(2)}) copy-start(f32[1,64,4096]{2,1,0:T(8,128)} %get-tuple-element.393) | copy-start | bytes 3145732 | tf_op jit(solution)/shard_map/while
  172.9 4.7 %copy-start = (f32[1,64,4096]{2,1,0:T(8,128)S(1)}, f32[1,64,4096]{2,1,0:T(8,128)}, u32[]{:S(2)}) copy-start(f32[1,64,4096]{2,1,0:T(8,128)} %get-tuple-element.393) | copy-start | bytes 3145732 | tf_op jit(solution)/shard_map/while
  203.1 51.8 %all-to-all-start = ((bf16[8,2,65536]{2,1,0:T(2,128)(2,1)}), bf16[8,2,65536]{2,1,0:T(2,128)(2,1)S(1)}, u32[]{:S(2)}, u32[]{:S(2)}) async-start(bf16[8,2,65536]{2,1,0:T(2,128)(2,1)} %reshape.29), calls=%async_computation | async-start | bytes 4194304 | tf_op jit(solution)/shard_map/all_to_all | solution.py:68
  268.0 0.8 copy-start.1
where the time goes:
time: 270 us; the launch traced here: 269 us
  other arithmetic  125 us (46%)
  waiting for transfers between devices  69 us (26%)
  local copies, waits for them, and re-layouts  44.4 us (16%)
  starting transfers between devices  17.2 us (6%)
  loops' own time  11.3 us (4%)
    all_to_all x1, waiting for transfers between devices, shards(): lax.all_to_all(partial_value[None], 'depth', split_axis=3, concat_axis=0,...  46.3 us
    add x8, other arithmetic, slice_step(): return acc + (1.0 - acc[3:4]) * placed  41.9 us
    another operation x16, other arithmetic, colour(): jnp.stack([shade * jax.nn.sigmoid(1.2 * cur + 0.2) * alpha, shade * jax.n...  26.2 us
    unnamed x12, local copies, waits for them, and re-layouts  25.9 us
    ppermute x2, waiting for transfers between devices, extended_2(): before = lax.ppermute(last, axis, up)  19.7 us
    while x16, other arithmetic  18.5 us
    convert_element_type x8, other arithmetic, slice_step(): block = lax.dynamic_slice_in_dim(extended, local, 3, 0).astype(jnp.float32)  15 us
    another operation x1, loops' own time, shards(): lax.fori_loop(0, slices, slice_step, jnp.zeros((4, rows, NY), jnp.float32))  11 us
  transfers between devices with their start and end apart: 5, of which 3 were waited for; matrix products, arithmetic and copies ran while one was open for 1% of the time, Pallas kernels for 0%

commit v1 on v0

--- a/solution.py
+++ b/solution.py
@@ -2,6 +2,7 @@
 import jax.numpy as jnp
 from jax import lax
 from jax.sharding import PartitionSpec as P
+from jax.lax import all_to_all, axis_size
 
 NY = 4096
 SMAX = 64
@@ -65,7 +66,10 @@
 
     acc = lax.fori_loop(0, slices, slice_step, jnp.zeros((4, rows, NY), jnp.float32))
     partial_value = acc.astype(jnp.bfloat16)
-    pieces = lax.all_to_all(partial_value[None], "depth", split_axis=3, concat_axis=0, tiled=True)
+    _link_field = lambda unit: jnp.concatenate(
+        all_to_all(jnp.stack(jnp.split(unit, axis_size("depth"), 3), axis=0), "depth", 0, 0), 0
+    )
+    pieces = _link_field(partial_value[None])
 
     def brick_step(position, image):
         source = jnp.where(flip, bricks - 1 - position, position).astype(jnp.int32)

time: 270 us -> 247 us (0.915)
  local copies, waits for them, and re-layouts: 44.4 us -> 22 us
    unnamed x12 -> x15, local copies, waits for them, and re-layouts: 25.9 us -> 8.33 us
    all_to_all x1 -> x0, local copies, waits for them, and re-layouts: 5.58 us -> none  [shards(): lax.all_to_all(partial_value[None], 'depth', split_axis=3, concat_axis=0,...]
  transfers between devices with their start and end apart: 5 -> 5, of which waited for: 3 -> 3; matrix products, arithmetic and copies ran while one was open for 1% -> 2% of each run, Pallas kernels for 0% -> 0%
where the time goes in v1:
time: 247 us; the launch traced here: 246 us
  other arithmetic  125 us (51%)
  waiting for transfers between devices  69 us (28%)
  local copies, waits for them, and re-layouts  22 us (9%)
  starting transfers between devices  17.2 us (7%)
  loops' own time  11.3 us (5%)
    all_to_all x1, waiting for transfers between devices, shards(): all_to_all(jnp.stack(jnp.split(unit, axis_size('depth'), 3), axis=0), 'de...  46.3 us
    add x8, other arithmetic, slice_step(): return acc + (1.0 - acc[3:4]) * placed  41.9 us
    another operation x16, other arithmetic, colour(): jnp.stack([shade * jax.nn.sigmoid(1.2 * cur + 0.2) * alpha, shade * jax.n...  26.2 us
    ppermute x2, waiting for transfers between devices, extended_2(): before = lax.ppermute(last, axis, up)  19.7 us
    while x16, other arithmetic  18.5 us
    convert_element_type x8, other arithmetic, slice_step(): block = lax.dynamic_slice_in_dim(extended, local, 3, 0).astype(jnp.float32)  15 us
    another operation x1, loops' own time, shards(): lax.fori_loop(0, slices, slice_step, jnp.zeros((4, rows, NY), jnp.float32))  11 us
    convert_element_type x8, other arithmetic, colour(): inside = ((column >= low) & (column < high)).astype(jnp.float32)  10.7 us
  transfers between devices with their start and end apart: 5, of which 3 were waited for; matrix products, arithmetic and copies ran while one was open for 2% of the time, Pallas kernels for 0%

profile of v1, /device:TPU:1, one launch (start us, length us, event | category | flops | bytes accessed | tf_op | source)
XLA Modules:
  0.0 246.4 jit_solution(7275596192450826629)
XLA Ops:
  1.3 4.0 %collective-permute-start = (bf16[1,64,4096]{2,1,0:T(8,128)(2,1)S(1)}, bf16[1,64,4096]{2,1,0:T(8,128)(2,1)S(1)}, u32[]{:S(2)}, u32[]{:S(2)}) collective-permute-start(bf16[1,64,4096]{2,1,0:T(8,128)(2,1)S(1)} %get-tuple-element.312), channel_id=1, source_target_pairs={{0,4},{4,8},{8,12},{12,16},{16,20},{20,24},{24,28},{1,5},{5,9},{9,... | collective-permute-start | bytes 1572872 | tf_op jit(solution)/shard_map/ppermute | solution.py:18
  7.3 19.7 %collective-permute-done = bf16[1,64,4096]{2,1,0:T(8,128)(2,1)S(1)} collective-permute-done((bf16[1,64,4096]{2,1,0:T(8,128)(2,1)S(1)}, bf16[1,64,4096]{2,1,0:T(8,128)(2,1)S(1)}, u32[]{:S(2)}, u32[]{:S(2)}) %collective-permute-start) | collective-permute-done | bytes 524320 | tf_op jit(solution)/shard_map/ppermute | solution.py:18
  30.0 4.6 %collective-permute-start.2 = (bf16[10,1,4096]{2,1,0:T(2,128)(2,1)S(1)}, bf16[10,1,4096]{2,1,0:T(2,128)(2,1)S(1)}, u32[]{:S(2)}, u32[]{:S(2)}) collective-permute-start(bf16[10,1,4096]{2,1,0:T(2,128)(2,1)S(1)} %get-tuple-element.309), channel_id=1, source_target_pairs={{0,1},{1,2},{2,3},{4,5},{5,6},{6,7},{8,9},{9,10},{10,11},{12,13},{... | collective-permute-start | bytes 245768 | tf_op jit(solution)/shard_map/ppermute | solution.py:18
  38.3 2.9 %collective-permute-done.3 = bf16[10,1,4096]{2,1,0:T(2,128)(2,1)S(1)} collective-permute-done((bf16[10,1,4096]{2,1,0:T(2,128)(2,1)S(1)}, bf16[10,1,4096]{2,1,0:T(2,128)(2,1)S(1)}, u32[]{:S(2)}, u32[]{:S(2)}) %collective-permute-start.3) | collective-permute-done | bytes 81952 | tf_op jit(solution)/shard_map/ppermute | solution.py:19
  41.2 6.1 %pad_maximum_fusion = bf16[10,66,4096]{2,1,0:T(8,128)(2,1)} fusion(bf16[10,1,4096]{2,1,0:T(2,128)(2,1)S(1)} %collective-permute-done.3, bf16[10,64,4096]{2,1,0:T(8,128)(2,1)S(1)} %constant_dynamic-update-slice_fusion, bf16[10,1,4096]{2,1,0:T(2,128)(2,1)S(1)} %collective-permute-done.2), kind=kLoop, calls=%fused_computation.53 | loop fusion | flops 16220160 | bytes 10813440 | tf_op jit(solution)/shard_map/concatenate | solution.py:20
  47.3 135.7 %while.30 = (s32[]{:T(128)}, f32[4,64,4096]{2,1,0:T(8,128)}, pred[]{:T(512)}, bf16[10,66,4096]{2,1,0:T(8,128)(2,1)}, s32[8]{0:T(128)S(1)}, /*index=5*/s32[1,2]{1...) while((s32[]{:T(128)}, f32[4,64,4096]{2,1,0:T(8,128)}, ...), condition=%wide.region_1.2_spmd.clone, body=%wide.region_0.1_spmd.clone.sunk | while | flops 30973964 | bytes 48940876 | solution.py:67
  49.4 2.5 %multiply_bitcast_fusion.5 = (f32[1,64,4096]{2,1,0:T(8,128)}, f32[64,4096]{1,0:T(8,128)S(1)}) fusion(f32[3,66,4096]{2,1,0:T(8,128)S(1)} %dynamic-slice_convert_fusion.2, f32[64,4096]{1,0:T(8,128)S(1)} %get-tuple-element.381), kind=kLoop, calls=%fused_computation.40.clone.1 | loop fusion | flops 8126464 | bytes 8388608 | tf_op jit(solution)/shard_map/while/body/eval_jaxpr/stack | solution.py:28
  57.0 3.9 %fusion.52 = f32[4,64,4096]{2,1,0:T(8,128)} fusion(s32[]{:T(128)S(6)} %select_n.74, f32[1,64,4096]{2,1,0:T(8,128)S(1)} %get-tuple-element.383, f32[1,64,4096]{2,1,0:T(8,128)S(1)} %get-tuple-element.384, f32[1,64,4096]{2,1,0:T(8,128)S(1)} %copy-done, f32[1,64,4096]{2,1,0:T(8,128)S(1)} %get-tuple-element.386, f32[4096]{0:T(1024)S(1)} %fusion.50, ...), kind=kLoop, calls=%fused_computation.10.clone.1 | loop fusion | flops 15728640 | bytes 13649408 | tf_op jit(solution)/shard_map/while/body/eval_jaxpr/add | solution.py:65
  63.1 2.5 %multiply_bitcast_fusion.5 = (f32[1,64,4096]{2,1,0:T(8,128)}, f32[64,4096]{1,0:T(8,128)S(1)}) fusion(f32[3,66,4096]{2,1,0:T(8,128)S(1)} %dynamic-slice_convert_fusion.2, f32[64,4096]{1,0:T(8,128)S(1)} %get-tuple-element.381), kind=kLoop, calls=%fused_computation.40.clone.1 | loop fusion | flops 8126464 | bytes 8388608 | tf_op jit(solution)/shard_map/while/body/eval_jaxpr/stack | solution.py:28
  68.2 2.6 %broadcast_select_fusion.4 = f32[4,64,4096]{2,1,0:T(8,128)S(1)} fusion(f32[4,64,4096]{2,1,0:T(8,128)} %get-tuple-element.407, pred[]{:T(512)S(6)} %compare.28), kind=kLoop, calls=%fused_computation.18.clone.2 | loop fusion | flops 1048576 | bytes 8388609 | tf_op jit(solution)/shard_map/while
  72.9 5.4 %fusion.52 = f32[4,64,4096]{2,1,0:T(8,128)} fusion(s32[]{:T(128)S(6)} %select_n.74, f32[1,64,4096]{2,1,0:T(8,128)S(1)} %get-tuple-element.383, f32[1,64,4096]{2,1,0:T(8,128)S(1)} %get-tuple-element.384, f32[1,64,4096]{2,1,0:T(8,128)S(1)} %copy-done, f32[1,64,4096]{2,1,0:T(8,128)S(1)} %get-tuple-element.386, f32[4096]{0:T(1024)S(1)} %fusion.50, ...), kind=kLoop, calls=%fused_computation.10.clone.1 | loop fusion | flops 15728640 | bytes 13649408 | tf_op jit(solution)/shard_map/while/body/eval_jaxpr/add | solution.py:65
  80.5 2.5 %multiply_bitcast_fusion.5 = (f32[1,64,4096]{2,1,0:T(8,128)}, f32[64,4096]{1,0:T(8,128)S(1)}) fusion(f32[3,66,4096]{2,1,0:T(8,128)S(1)} %dynamic-slice_convert_fusion.2, f32[64,4096]{1,0:T(8,128)S(1)} %get-tuple-element.381), kind=kLoop, calls=%fused_computation.40.clone.1 | loop fusion | flops 8126464 | bytes 8388608 | tf_op jit(solution)/shard_map/while/body/eval_jaxpr/stack | solution.py:28
  85.7 2.6 %broadcast_select_fusion.4 = f32[4,64,4096]{2,1,0:T(8,128)S(1)} fusion(f32[4,64,4096]{2,1,0:T(8,128)} %get-tuple-element.407, pred[]{:T(512)S(6)} %compare.28), kind=kLoop, calls=%fused_computation.18.clone.2 | loop fusion | flops 1048576 | bytes 8388609 | tf_op jit(solution)/shard_map/while
  90.3 5.4 %fusion.52 = f32[4,64,4096]{2,1,0:T(8,128)} fusion(s32[]{:T(128)S(6)} %select_n.74, f32[1,64,4096]{2,1,0:T(8,128)S(1)} %get-tuple-element.383, f32[1,64,4096]{2,1,0:T(8,128)S(1)} %get-tuple-element.384, f32[1,64,4096]{2,1,0:T(8,128)S(1)} %copy-done, f32[1,64,4096]{2,1,0:T(8,128)S(1)} %get-tuple-element.386, f32[4096]{0:T(1024)S(1)} %fusion.50, ...), kind=kLoop, calls=%fused_computation.10.clone.1 | loop fusion | flops 15728640 | bytes 13649408 | tf_op jit(solution)/shard_map/while/body/eval_jaxpr/add | solution.py:65
  97.9 2.5 %multiply_bitcast_fusion.5 = (f32[1,64,4096]{2,1,0:T(8,128)}, f32[64,4096]{1,0:T(8,128)S(1)}) fusion(f32[3,66,4096]{2,1,0:T(8,128)S(1)} %dynamic-slice_convert_fusion.2, f32[64,4096]{1,0:T(8,128)S(1)} %get-tuple-element.381), kind=kLoop, calls=%fused_computation.40.clone.1 | loop fusion | flops 8126464 | bytes 8388608 | tf_op jit(solution)/shard_map/while/body/eval_jaxpr/stack | solution.py:28
  103.1 2.6 %broadcast_select_fusion.4 = f32[4,64,4096]{2,1,0:T(8,128)S(1)} fusion(f32[4,64,4096]{2,1,0:T(8,128)} %get-tuple-element.407, pred[]{:T(512)S(6)} %compare.28), kind=kLoop, calls=%fused_computation.18.clone.2 | loop fusion | flops 1048576 | bytes 8388609 | tf_op jit(solution)/shard_map/while
  107.8 5.4 %fusion.52 = f32[4,64,4096]{2,1,0:T(8,128)} fusion(s32[]{:T(128)S(6)} %select_n.74, f32[1,64,4096]{2,1,0:T(8,128)S(1)} %get-tuple-element.383, f32[1,64,4096]{2,1,0:T(8,128)S(1)} %get-tuple-element.384, f32[1,64,4096]{2,1,0:T(8,128)S(1)} %copy-done, f32[1,64,4096]{2,1,0:T(8,128)S(1)} %get-tuple-element.386, f32[4096]{0:T(1024)S(1)} %fusion.50, ...), kind=kLoop, calls=%fused_computation.10.clone.1 | loop fusion | flops 15728640 | bytes 13649408 | tf_op jit(solution)/shard_map/while/body/eval_jaxpr/add | solution.py:65
  115.4 2.5 %multiply_bitcast_fusion.5 = (f32[1,64,4096]{2,1,0:T(8,128)}, f32[64,4096]{1,0:T(8,128)S(1)}) fusion(f32[3,66,4096]{2,1,0:T(8,128)S(1)} %dynamic-slice_convert_fusion.2, f32[64,4096]{1,0:T(8,128)S(1)} %get-tuple-element.381), kind=kLoop, calls=%fused_computation.40.clone.1 | loop fusion | flops 8126464 | bytes 8388608 | tf_op jit(solution)/shard_map/while/body/eval_jaxpr/stack | solution.py:28
  120.6 2.6 %broadcast_select_fusion.4 = f32[4,64,4096]{2,1,0:T(8,128)S(1)} fusion(f32[4,64,4096]{2,1,0:T(8,128)} %get-tuple-element.407, pred[]{:T(512)S(6)} %compare.28), kind=kLoop, calls=%fused_computation.18.clone.2 | loop fusion | flops 1048576 | bytes 8388609 | tf_op jit(solution)/shard_map/while
  125.2 5.4 %fusion.52 = f32[4,64,4096]{2,1,0:T(8,128)} fusion(s32[]{:T(128)S(6)} %select_n.74, f32[1,64,4096]{2,1,0:T(8,128)S(1)} %get-tuple-element.383, f32[1,64,4096]{2,1,0:T(8,128)S(1)} %get-tuple-element.384, f32[1,64,4096]{2,1,0:T(8,128)S(1)} %copy-done, f32[1,64,4096]{2,1,0:T(8,128)S(1)} %get-tuple-element.386, f32[4096]{0:T(1024)S(1)} %fusion.50, ...), kind=kLoop, calls=%fused_computation.10.clone.1 | loop fusion | flops 15728640 | bytes 13649408 | tf_op jit(solution)/shard_map/while/body/eval_jaxpr/add | solution.py:65
  132.8 2.5 %multiply_bitcast_fusion.5 = (f32[1,64,4096]{2,1,0:T(8,128)}, f32[64,4096]{1,0:T(8,128)S(1)}) fusion(f32[3,66,4096]{2,1,0:T(8,128)S(1)} %dynamic-slice_convert_fusion.2, f32[64,4096]{1,0:T(8,128)S(1)} %get-tuple-element.381), kind=kLoop, calls=%fused_computation.40.clone.1 | loop fusion | flops 8126464 | bytes 8388608 | tf_op jit(solution)/shard_map/while/body/eval_jaxpr/stack | solution.py:28
  138.0 2.6 %broadcast_select_fusion.4 = f32[4,64,4096]{2,1,0:T(8,128)S(1)} fusion(f32[4,64,4096]{2,1,0:T(8,128)} %get-tuple-element.407, pred[]{:T(512)S(6)} %compare.28), kind=kLoop, calls=%fused_computation.18.clone.2 | loop fusion | flops 1048576 | bytes 8388609 | tf_op jit(solution)/shard_map/while
  142.7 5.4 %fusion.52 = f32[4,64,4096]{2,1,0:T(8,128)} fusion(s32[]{:T(128)S(6)} %select_n.74, f32[1,64,4096]{2,1,0:T(8,128)S(1)} %get-tuple-element.383, f32[1,64,4096]{2,1,0:T(8,128)S(1)} %get-tuple-element.384, f32[1,64,4096]{2,1,0:T(8,128)S(1)} %copy-done, f32[1,64,4096]{2,1,0:T(8,128)S(1)} %get-tuple-element.386, f32[4096]{0:T(1024)S(1)} %fusion.50, ...), kind=kLoop, calls=%fused_computation.10.clone.1 | loop fusion | flops 15728640 | bytes 13649408 | tf_op jit(solution)/shard_map/while/body/eval_jaxpr/add | solution.py:65
  150.3 2.5 %multiply_bitcast_fusion.5 = (f32[1,64,4096]{2,1,0:T(8,128)}, f32[64,4096]{1,0:T(8,128)S(1)}) fusion(f32[3,66,4096]{2,1,0:T(8,128)S(1)} %dynamic-slice_convert_fusion.2, f32[64,4096]{1,0:T(8,128)S(1)} %get-tuple-element.381), kind=kLoop, calls=%fused_computation.40.clone.1 | loop fusion | flops 8126464 | bytes 8388608 | tf_op jit(solution)/shard_map/while/body/eval_jaxpr/stack | solution.py:28
  155.5 2.6 %broadcast_select_fusion.4 = f32[4,64,4096]{2,1,0:T(8,128)S(1)} fusion(f32[4,64,4096]{2,1,0:T(8,128)} %get-tuple-element.407, pred[]{:T(512)S(6)} %compare.28), kind=kLoop, calls=%fused_computation.18.clone.2 | loop fusion | flops 1048576 | bytes 8388609 | tf_op jit(solution)/shard_map/while
  160.1 5.4 %fusion.52 = f32[4,64,4096]{2,1,0:T(8,128)} fusion(s32[]{:T(128)S(6)} %select_n.74, f32[1,64,4096]{2,1,0:T(8,128)S(1)} %get-tuple-element.383, f32[1,64,4096]{2,1,0:T(8,128)S(1)} %get-tuple-element.384, f32[1,64,4096]{2,1,0:T(8,128)S(1)} %copy-done, f32[1,64,4096]{2,1,0:T(8,128)S(1)} %get-tuple-element.386, f32[4096]{0:T(1024)S(1)} %fusion.50, ...), kind=kLoop, calls=%fused_computation.10.clone.1 | loop fusion | flops 15728640 | bytes 13649408 | tf_op jit(solution)/shard_map/while/body/eval_jaxpr/add | solution.py:65
  167.7 2.5 %multiply_bitcast_fusion.5 = (f32[1,64,4096]{2,1,0:T(8,128)}, f32[64,4096]{1,0:T(8,128)S(1)}) fusion(f32[3,66,4096]{2,1,0:T(8,128)S(1)} %dynamic-slice_convert_fusion.2, f32[64,4096]{1,0:T(8,128)S(1)} %get-tuple-element.381), kind=kLoop, calls=%fused_computation.40.clone.1 | loop fusion | flops 8126464 | bytes 8388608 | tf_op jit(solution)/shard_map/while/body/eval_jaxpr/stack | solution.py:28
  172.9 2.6 %broadcast_select_fusion.4 = f32[4,64,4096]{2,1,0:T(8,128)S(1)} fusion(f32[4,64,4096]{2,1,0:T(8,128)} %get-tuple-element.407, pred[]{:T(512)S(6)} %compare.28), kind=kLoop, calls=%fused_computation.18.clone.2 | loop fusion | flops 1048576 | bytes 8388609 | tf_op jit(solution)/shard_map/while
  177.6 5.4 %fusion.52 = f32[4,64,4096]{2,1,0:T(8,128)} fusion(s32[]{:T(128)S(6)} %select_n.74, f32[1,64,4096]{2,1,0:T(8,128)S(1)} %get-tuple-element.383, f32[1,64,4096]{2,1,0:T(8,128)S(1)} %get-tuple-element.384, f32[1,64,4096]{2,1,0:T(8,128)S(1)} %copy-done, f32[1,64,4096]{2,1,0:T(8,128)S(1)} %get-tuple-element.386, f32[4096]{0:T(1024)S(1)} %fusion.50, ...), kind=kLoop, calls=%fused_computation.10.clone.1 | loop fusion | flops 15728640 | bytes 13649408 | tf_op jit(solution)/shard_map/while/body/eval_jaxpr/add | solution.py:65
  191.2 5.5 %all-to-all-start = ((bf16[8,1,4,64,512]{4,3,2,1,0:T(8,128)(2,1)}), bf16[8,1,4,64,512]{4,3,2,1,0:T(8,128)(2,1)S(1)}, u32[]{:S(2)}, u32[]{:S(2)}) async-start(bf16[8,1,4,64,512]{4,3,2,1,0:T(8,128)(2,1)} %fusion.28), calls=%async_computation | async-start | bytes 4194304 | tf_op jit(solution)/shard_map/all_to_all | solution.py:70
  196.7 46.3 %all-to-all-done = bf16[8,1,4,64,512]{4,3,2,1,0:T(8,128)(2,1)S(1)} async-done(((bf16[8,1,4,64,512]{4,3,2,1,0:T(8,128)(2,1)}), bf16[8,1,4,64,512]{4,3,2,1,0:T(8,128)(2,1)S(1)}, u32[]{:S(2)}, u32[]{:S(2)}) %all-to-all-start) | async-done | bytes 2097184 | tf_op jit(solution)/shard_map/all_to_all | solution.py:70
  243.1 2.5 %while.31 = (s32[]{:T(128)}, f32[4,64,512]{2,1,0:T(8,128)S(1)}, pred[]{:T(512)}, bf16[8,4,64,512]{3,2,1,0:T(8,128)(2,1)S(1)}, s32[]{:T(128)}, /*index=5*/s32[]{:T(128)}, s32[]{:T(128)}, s32[]{:T(128)}) while((s32[]{:T(128)}, f32[4,64,512]{2,1,0:T(8,128)S(1)}, pred[]{:T(512)}, bf16[8,4,64,512]{3,2,1,0:T(8,128)(2,1)S(1)}, s32[]{:T(128)}, ...), condition=%wide.region_3.4_spmd.clone, body=%wide.region_2.3_spmd.clone.sunk | while | flops 688136 | bytes 2752671 | solution.py:80
  (125 shorter events, 64.6 us)
Async XLA Ops:
  1.3 25.8 %collective-permute-start = (bf16[1,64,4096]{2,1,0:T(8,128)(2,1)S(1)}, bf16[1,64,4096]{2,1,0:T(8,128)(2,1)S(1)}, u32[]{:S(2)}, u32[]{:S(2)}) collective-permute-start(bf16[1,64,4096]{2,1,0:T(8,128)(2,1)S(1)} %get-tuple-element.312), channel_id=1, source_target_pairs={{0,4},{4,8},{8,12},{12,16},{16,20},{20,24},{24,28},{1,5},{5,9},{9,... | collective-permute-start | bytes 1572872 | tf_op jit(solution)/shard_map/ppermute | solution.py:18
  5.2 24.3 %collective-permute-start.1 = (bf16[1,64,4096]{2,1,0:T(8,128)(2,1)S(1)}, bf16[1,64,4096]{2,1,0:T(8,128)(2,1)S(1)}, u32[]{:S(2)}, u32[]{:S(2)}) collective-permute-start(bf16[1,64,4096]{2,1,0:T(8,128)(2,1)S(1)} %get-tuple-element.311), channel_id=1, source_target_pairs={{4,0},{8,4},{12,8},{16,12},{20,16},{24,20},{28,24},{5,1},{9,5},{13... | collective-permute-start | bytes 1572872 | tf_op jit(solution)/shard_map/ppermute | solution.py:19
  27.1 9.4 %copy-start.3 = (s32[64]{0:T(128)S(1)}, s32[64]{0:T(128)}, u32[]{:S(2)}) copy-start(s32[64]{0:T(128)} %param.8) | copy-start | bytes 772
  30.0 8.3 %collective-permute-start.2 = (bf16[10,1,4096]{2,1,0:T(2,128)(2,1)S(1)}, bf16[10,1,4096]{2,1,0:T(2,128)(2,1)S(1)}, u32[]{:S(2)}, u32[]{:S(2)}) collective-permute-start(bf16[10,1,4096]{2,1,0:T(2,128)(2,1)S(1)} %get-tuple-element.309), channel_id=1, source_target_pairs={{0,1},{1,2},{2,3},{4,5},{5,6},{6,7},{8,9},{9,10},{10,11},{12,13},{... | collective-permute-start | bytes 245768 | tf_op jit(solution)/shard_map/ppermute | solution.py:18
  34.5 6.6 %collective-permute-start.3 = (bf16[10,1,4096]{2,1,0:T(2,128)(2,1)S(1)}, bf16[10,1,4096]{2,1,0:T(2,128)(2,1)S(1)}, u32[]{:S(2)}, u32[]{:S(2)}) collective-permute-start(bf16[10,1,4096]{2,1,0:T(2,128)(2,1)S(1)} %get-tuple-element.310), channel_id=1, source_target_pairs={{1,0},{2,1},{3,2},{5,4},{6,5},{7,6},{9,8},{10,9},{11,10},{13,12},{... | collective-permute-start | bytes 245768 | tf_op jit(solution)/shard_map/ppermute | solution.py:19
  38.3 9.0 %copy-start.2 = (s32[1,2]{1,0:T(1,128)S(1)}, s32[1,2]{1,0:T(1,128)}, u32[]{:S(2)}) copy-start(s32[1,2]{1,0:T(1,128)} %param.9) | copy-start | bytes 28
  54.6 2.4 copy-start
  68.2 4.7 %copy-start = (f32[1,64,4096]{2,1,0:T(8,128)S(1)}, f32[1,64,4096]{2,1,0:T(8,128)}, u32[]{:S(2)}) copy-start(f32[1,64,4096]{2,1,0:T(8,128)} %get-tuple-element.385) | copy-start | bytes 3145732 | tf_op jit(solution)/shard_map/while
  85.7 4.7 %copy-start = (f32[1,64,4096]{2,1,0:T(8,128)S(1)}, f32[1,64,4096]{2,1,0:T(8,128)}, u32[]{:S(2)}) copy-start(f32[1,64,4096]{2,1,0:T(8,128)} %get-tuple-element.385) | copy-start | bytes 3145732 | tf_op jit(solution)/shard_map/while
  103.1 4.7 %copy-start = (f32[1,64,4096]{2,1,0:T(8,128)S(1)}, f32[1,64,4096]{2,1,0:T(8,128)}, u32[]{:S(2)}) copy-start(f32[1,64,4096]{2,1,0:T(8,128)} %get-tuple-element.385) | copy-start | bytes 3145732 | tf_op jit(solution)/shard_map/while
  120.6 4.7 %copy-start = (f32[1,64,4096]{2,1,0:T(8,128)S(1)}, f32[1,64,4096]{2,1,0:T(8,128)}, u32[]{:S(2)}) copy-start(f32[1,64,4096]{2,1,0:T(8,128)} %get-tuple-element.385) | copy-start | bytes 3145732 | tf_op jit(solution)/shard_map/while
  138.0 4.7 %copy-start = (f32[1,64,4096]{2,1,0:T(8,128)S(1)}, f32[1,64,4096]{2,1,0:T(8,128)}, u32[]{:S(2)}) copy-start(f32[1,64,4096]{2,1,0:T(8,128)} %get-tuple-element.385) | copy-start | bytes 3145732 | tf_op jit(solution)/shard_map/while
  155.4 4.7 %copy-start = (f32[1,64,4096]{2,1,0:T(8,128)S(1)}, f32[1,64,4096]{2,1,0:T(8,128)}, u32[]{:S(2)}) copy-start(f32[1,64,4096]{2,1,0:T(8,128)} %get-tuple-element.385) | copy-start | bytes 3145732 | tf_op jit(solution)/shard_map/while
  172.9 4.7 %copy-start = (f32[1,64,4096]{2,1,0:T(8,128)S(1)}, f32[1,64,4096]{2,1,0:T(8,128)}, u32[]{:S(2)}) copy-start(f32[1,64,4096]{2,1,0:T(8,128)} %get-tuple-element.385) | copy-start | bytes 3145732 | tf_op jit(solution)/shard_map/while
  191.2 51.8 %all-to-all-start = ((bf16[8,1,4,64,512]{4,3,2,1,0:T(8,128)(2,1)}), bf16[8,1,4,64,512]{4,3,2,1,0:T(8,128)(2,1)S(1)}, u32[]{:S(2)}, u32[]{:S(2)}) async-start(bf16[8,1,4,64,512]{4,3,2,1,0:T(8,128)(2,1)} %fusion.28), calls=%async_computation | async-start | bytes 4194304 | tf_op jit(solution)/shard_map/all_to_all | solution.py:70
  245.6 0.8 copy-start.1
